TPU v7x, 32 devices: a whole 2x2x4 slice. The times are simulated.
32 devices in a mesh: row: 4 (over y, x), col: 8 (over z, core).
Axes of the slice: x: 2, y: 2, z: 4, core: 2. Of those that a mesh axis runs over, the one named last changes fastest.
Arguments:
- x_iterate: float32 [2048, 2048], P('row', 'col'), may hold values from -6 to 6
- z_inverse: float32 [2048, 2048], P('row', 'col'), may hold values from -0.25 to 0.25
- edge_src: int32 [8, 8, 64], P('row', 'col'), may hold values from 0 to 255
- edge_dst: int32 [8, 8, 64], P('row', 'col'), may hold values from 0 to 255
- edge_count: int32 [8, 8], P('row', 'col'), may hold values from 1 to 64, as said below
Outputs:
- schur_row: float32 [8, 8, 64], P('row', 'col')
Inputs may be any that keep to these rules, and one draw needn't show every extreme that they name: `edge_count`: slots at and beyond a block pair's count are ignored; some block pair has all 64 slots live in every draw.
All inputs are finite; a program needn't handle non-finite values.
Results may differ from a plain program's by a relative error of at most 0.0001.
Values sent between devices are 32-bit elements; how exact they have to be, the bound alone decides.
No kernel may reach another device: no remote copies, remote signals or barrier semaphores. Data moves between devices by JAX's collectives and lax.ppermute only.
A program may use at most 64 MiB of HBM per device.

v0:
```python
import functools

import jax
import jax.numpy as jnp
from jax import lax
from jax.experimental import pallas as pl
from jax.experimental.pallas import tpu as pltpu
from jax.sharding import PartitionSpec as P


AXES = ("row", "col")
VMEM = pl.BlockSpec(memory_space=pltpu.VMEM)
PARAMS = pltpu.CompilerParams(vmem_limit_bytes=8 * 2**20)


def terms_of(side):
    split = ([], [])
    for a in range(2):
        for s in range(2):
            total = a + side + s
            split[total // 2 != side].append((a, total % 2))
    return split


def send(shard, dest):
    n_row, n_col = lax.axis_size("row"), lax.axis_size("col")
    pairs = []
    for r in range(n_row):
        for c in range(n_col):
            to_r, to_pair, to_side = dest(r, c // 2, c % 2)
            to_c = to_pair * 2 + to_side
            pairs.append((r * n_col + c, to_r % n_row * n_col + to_c % n_col))
    return lax.ppermute(shard, AXES, pairs)


def swap(shard):
    return send(shard, lambda r, pair, side: (r, pair, 1 - side))


def pieces(value):
    high = value.astype(jnp.bfloat16)
    rest = value - high.astype(jnp.float32)
    middle = rest.astype(jnp.bfloat16)
    low = (rest - middle.astype(jnp.float32)).astype(jnp.bfloat16)
    return high, middle, low


def diagonal(slots):
    return lax.broadcasted_iota(jnp.int32, (slots, slots), 0) == lax.broadcasted_iota(jnp.int32, (slots, slots), 1)


def eye_kernel(eye_ref):
    eye_ref[...] = diagonal(eye_ref.shape[0]).astype(jnp.float32)


def pick(lines, width, eye):
    columns = []
    for line in lines:
        slots = line.shape[1]
        spread = jnp.where(eye, jnp.broadcast_to(line, (slots, slots)), 0)
        columns.append(jnp.sum(spread, axis=1, keepdims=True))
    column = jnp.concatenate(columns, axis=0)
    chosen = column == lax.broadcasted_iota(jnp.int32, (column.shape[0], width), 1)
    return chosen.astype(jnp.float32).astype(jnp.bfloat16)


def by_side(action):
    here = lax.axis_index("col") % 2
    for side in range(2):
        pl.when(here == side)(functools.partial(action, side))


def gather_kernel(spare, of_x, index_ref, own_ref, partner_ref, eye_ref, out_ref):
    width = out_ref.shape[1]
    slots = index_ref.shape[2]
    eye = eye_ref[...] > 0

    @by_side
    def _(side):
        blocks = {}
        for place, (a, g) in enumerate(terms_of(1 - side)[spare]):
            blocks.setdefault((g != side, a) if of_x else (True, g), []).append((place, a))
        for (partner, at), wanted in blocks.items():
            chosen = pick([index_ref[a] for _, a in wanted], width, eye)
            block = (partner_ref if partner else own_ref)[at * width : (at + 1) * width, :]
            taken = sum(
                lax.dot_general(
                    chosen, piece, (((1,), (0 if of_x else 1,)), ((), ())), preferred_element_type=jnp.float32
                )
                for piece in pieces(block)
            )
            for n, (place, _) in enumerate(wanted):
                out_ref[place * slots : (place + 1) * slots, :] = taken[n * slots : (n + 1) * slots]


def line(values, eye):
    slots = eye.shape[0]
    spread = jnp.where(eye, jnp.broadcast_to(jnp.sum(values, axis=1, keepdims=True), (slots, slots)), 0.0)
    return jnp.sum(spread, axis=0, keepdims=True)


def finish_kernel(x_main, x_spare, z_main, z_spare, count_ref, eye_ref, out_ref):
    slots = out_ref.shape[2]
    slot = lax.broadcasted_iota(jnp.int32, (1, slots), 1)
    eye = eye_ref[...] > 0

    @by_side
    def _(side):
        for a in range(2):
            products = []
            for terms, x_ref, z_ref in zip(terms_of(side), (x_main, x_spare), (z_main, z_spare)):
                for n, term in enumerate(terms):
                    if term[0] == a:
                        at = slice(n * slots, (n + 1) * slots)
                        products.append(x_ref[at, :] * z_ref[at, :])
            out_ref[a] = jnp.where(slot < count_ref[a], line(sum(products[1:], products[0]), eye), 0.0)


def call(kernel, shapes, *operands, cost=None):
    return pl.pallas_call(
        kernel,
        out_shape=[jax.ShapeDtypeStruct(shape, jnp.float32) for shape in shapes],
        in_specs=[VMEM] * len(operands),
        out_specs=[VMEM] * len(shapes),
        compiler_params=PARAMS,
        cost_estimate=cost,
    )(*operands)


def body(x_iterate, z_inverse, edge_src, edge_dst, edge_count):
    width = x_iterate.shape[1]
    slots = edge_src.shape[2]
    assert x_iterate.shape[0] == 2 * width
    x_partner = swap(x_iterate)
    z_partner = swap(z_inverse)
    (eye,) = call(eye_kernel, [(slots, slots)], cost=pl.CostEstimate(flops=2 * 10**9, bytes_accessed=16384, transcendentals=0))

    def request_x(spare):
        return lambda r, pair, side: (r, pair + r + (side ^ spare), 1 - side)

    def reply_x(spare):
        return lambda r, pair, side: (r, pair - r - (1 - side ^ spare), 1 - side)

    def request_z(spare):
        return lambda r, pair, side: (r + pair + (side ^ spare), pair, 1 - side)

    def reply_z(spare):
        return lambda r, pair, side: (r - pair - (1 - side ^ spare), pair, 1 - side)

    x_got, z_got = [], []
    for spare in range(2):
        shape = [(len(terms_of(0)[spare]) * slots, width)]
        src = send(edge_src, request_x(spare))
        (rows,) = call(functools.partial(gather_kernel, spare, True), shape, src, x_iterate, x_partner, eye)
        x_got.append(send(rows, reply_x(spare)))
        dst = send(edge_dst, request_z(spare))
        (columns,) = call(functools.partial(gather_kernel, spare, False), shape, dst, eye, z_partner, eye)
        z_got.append(send(columns, reply_z(spare)))
    count = edge_count.reshape(2, 1, 1)
    (out,) = call(finish_kernel, [(2, 1, slots)], *x_got, *z_got, count, eye)
    return out


def solution(mesh):
    return jax.shard_map(
        body,
        mesh=mesh,
        in_specs=(
            P("row", "col"),
            P("row", "col"),
            P("row", "col", None),
            P("row", "col", None),
            P("row", "col"),
        ),
        out_specs=P("row", "col", None),
        check_vma=False,
    )
```

profile of v0, /device:TPU:4, one launch (start us, length us, event | category | flops | bytes accessed | tf_op | source)
XLA Modules:
  0.0 24.7 jit_solution(13297699737941552994)
XLA Ops:
  0.0 0.0 collective-permute-start.6
  0.0 0.5 %collective-permute-start.1 = (f32[512,256]{1,0:T(8,128)}, f32[512,256]{1,0:T(8,128)S(1)}, u32[]{:S(2)}, u32[]{:S(2)}) collective-permute-start(f32[512,256]{1,0:T(8,128)} %own_ref.3), channel_id=1, source_target_pairs={{0,1},{1,0},{2,3},{3,2},{4,5},{5,4},{6,7},{7,6},{8,9},{9,8},{10,11... | collective-permute-start | bytes 1572872 | tf_op jit(solution)/shard_map/ppermute | solution.py:33
  0.5 2.2 %collective-permute-start = (s32[2,1,64]{2,1,0:T(1,128)}, s32[2,1,64]{2,1,0:T(1,128)S(1)}, u32[]{:S(2)}, u32[]{:S(2)}) collective-permute-start(s32[2,1,64]{2,1,0:T(1,128)} %param.7), channel_id=1, source_target_pairs={{0,1},{1,2},{2,3},{3,4},{4,5},{5,6},{6,7},{7,0},{8,11},{9,12},{10,... | collective-permute-start | bytes 1544 | tf_op jit(solution)/shard_map/ppermute | solution.py:33
  2.7 1.5 %collective-permute-start.5 = (s32[2,1,64]{2,1,0:T(1,128)}, s32[2,1,64]{2,1,0:T(1,128)S(1)}, u32[]{:S(2)}, u32[]{:S(2)}) collective-permute-start(s32[2,1,64]{2,1,0:T(1,128)} %param.8), channel_id=1, source_target_pairs={{0,1},{1,8},{2,11},{3,18},{4,21},{5,28},{6,31},{7,6},{8,9},{9,16},... | collective-permute-start | bytes 1544 | tf_op jit(solution)/shard_map/ppermute | solution.py:33
  4.2 0.0 copy-start
  4.2 2.6 %collective-permute-done.5.index_ref = s32[2,1,64]{2,1,0:T(1,128)S(1)} collective-permute-done((s32[2,1,64]{2,1,0:T(1,128)}, s32[2,1,64]{2,1,0:T(1,128)S(1)}, u32[]{:S(2)}, u32[]{:S(2)}) %collective-permute-start.5) | collective-permute-done | bytes 544 | tf_op jit(solution)/shard_map/ppermute | solution.py:33
  6.8 0.0 collective-permute-done.6.partner_ref
  6.8 0.5 %shard_map.58 = f32[192,256]{1,0:T(8,128)S(1)} custom-call(s32[2,1,64]{2,1,0:T(1,128)S(1)} %collective-permute-done.5.index_ref, f32[64,64]{1,0:T(8,128)S(1)} %shard_map.55.eye_ref.own_ref, f32[512,256]{1,0:T(8,128)S(1)} %collective-permute-done.6.partner_ref, f32[64,64]{1,0:T(8,128)S(1)} %shard_map.55.eye_ref.own_ref), custom_call_target="tpu_custom_call" | custom-call | tf_op jit(solution)/shard_map/pallas_call | solution.py:120
  7.4 0.0 copy-start.1
  7.4 0.0 copy-start.2
  7.4 0.1 collective-permute-start.7
  7.4 0.0 collective-permute-done.index_ref
  7.5 0.0 collective-permute-done.1.partner_ref
  7.5 0.0 copy-done
  7.5 0.4 %shard_map.56 = f32[192,256]{1,0:T(8,128)S(1)} custom-call(s32[2,1,64]{2,1,0:T(1,128)S(1)} %collective-permute-done.index_ref, f32[512,256]{1,0:T(8,128)S(1)} %copy-done, f32[512,256]{1,0:T(8,128)S(1)} %collective-permute-done.1.partner_ref, f32[64,64]{1,0:T(8,128)S(1)} %shard_map.55.eye_ref.own_ref), custom_call_target="tpu_custom_call" | custom-call | tf_op jit(solution)/shard_map/pallas_call | solution.py:120
  7.9 0.8 %collective-permute-start.2 = (f32[192,256]{1,0:T(8,128)S(1)}, f32[192,256]{1,0:T(8,128)S(1)}, u32[]{:S(2)}, u32[]{:S(2)}) collective-permute-start(f32[192,256]{1,0:T(8,128)S(1)} %shard_map.56), channel_id=1, source_target_pairs={{0,7},{1,0},{2,1},{3,2},{4,3},{5,4},{6,5},{7,6},{8,13},{9,14},{10,... | collective-permute-start | bytes 589832 | tf_op jit(solution)/shard_map/ppermute | solution.py:33
  8.7 0.0 copy-done.1
  8.7 1.7 %collective-permute-start.8 = (s32[2,1,64]{2,1,0:T(1,128)S(1)}, s32[2,1,64]{2,1,0:T(1,128)S(1)}, u32[]{:S(2)}, u32[]{:S(2)}) collective-permute-start(s32[2,1,64]{2,1,0:T(1,128)S(1)} %copy-done.1), channel_id=1, source_target_pairs={{0,9},{1,0},{2,19},{3,10},{4,29},{5,20},{6,7},{7,30},{8,17},{9,8},... | collective-permute-start | bytes 1544 | tf_op jit(solution)/shard_map/ppermute | solution.py:33
  10.4 0.0 copy-done.2
  10.4 1.8 %collective-permute-start.3 = (s32[2,1,64]{2,1,0:T(1,128)S(1)}, s32[2,1,64]{2,1,0:T(1,128)S(1)}, u32[]{:S(2)}, u32[]{:S(2)}) collective-permute-start(s32[2,1,64]{2,1,0:T(1,128)S(1)} %copy-done.2), channel_id=1, source_target_pairs={{0,3},{1,0},{2,5},{3,2},{4,7},{5,4},{6,1},{7,6},{8,13},{9,10},{10,... | collective-permute-start | bytes 1544 | tf_op jit(solution)/shard_map/ppermute | solution.py:33
  12.3 0.0 collective-permute-done.8.index_ref
  12.3 0.2 shard_map.59
  12.5 1.4 %collective-permute-start.9 = (f32[64,256]{1,0:T(8,128)S(1)}, f32[64,256]{1,0:T(8,128)S(1)}, u32[]{:S(2)}, u32[]{:S(2)}) collective-permute-start(f32[64,256]{1,0:T(8,128)S(1)} %shard_map.59), channel_id=1, source_target_pairs={{0,1},{1,24},{2,27},{3,18},{4,21},{5,12},{6,15},{7,6},{8,9},{9,0},... | collective-permute-start | bytes 196616 | tf_op jit(solution)/shard_map/ppermute | solution.py:33
  13.9 4.3 %collective-permute-done.3.index_ref = s32[2,1,64]{2,1,0:T(1,128)S(1)} collective-permute-done((s32[2,1,64]{2,1,0:T(1,128)S(1)}, s32[2,1,64]{2,1,0:T(1,128)S(1)}, u32[]{:S(2)}, u32[]{:S(2)}) %collective-permute-start.3) | collective-permute-done | bytes 544 | tf_op jit(solution)/shard_map/ppermute | solution.py:33
  18.2 0.2 shard_map.57
  18.5 0.0 copy-start.3
  18.5 0.1 collective-permute-start.4
  18.5 0.6 %copy-done.3 = s32[2,1]{0,1:T(1,128)S(1)} copy-done((s32[2,1]{0,1:T(1,128)S(1)}, s32[2,1]{0,1:T(1,128)}, u32[]{:S(2)}) %copy-start.3) | copy-done | bytes 32
  19.1 0.1 copy.6.count_ref
  19.2 0.0 collective-permute-done.9.z_spare
  19.2 4.8 %collective-permute-done.4.x_spare = f32[64,256]{1,0:T(8,128)S(1)} collective-permute-done((f32[64,256]{1,0:T(8,128)S(1)}, f32[64,256]{1,0:T(8,128)S(1)}, u32[]{:S(2)}, u32[]{:S(2)}) %collective-permute-start.4) | collective-permute-done | bytes 65568 | tf_op jit(solution)/shard_map/ppermute | solution.py:33
  24.0 0.0 collective-permute-done.7.z_main
  24.0 0.0 collective-permute-done.2.x_main
  24.0 0.7 %shard_map.60 = f32[2,1,64]{2,1,0:T(1,128)} custom-call(f32[192,256]{1,0:T(8,128)S(1)} %collective-permute-done.2.x_main, f32[64,256]{1,0:T(8,128)S(1)} %collective-permute-done.4.x_spare, f32[192,256]{1,0:T(8,128)S(1)} %collective-permute-done.7.z_main, f32[64,256]{1,0:T(8,128)S(1)} %collective-permute-done.9.z_spare, s32[2,1,1]{2,1,0:T(1,128)S(1)} %copy.6.count_ref, ...), custom_call_target="tpu_custom_call" | custom-call | tf_op jit(solution)/shard_map/pallas_call | solution.py:120
  (1 shorter events, 0.0 us)
Async XLA Ops:
  0.0 6.8 %collective-permute-start.6 = (f32[512,256]{1,0:T(8,128)}, f32[512,256]{1,0:T(8,128)S(1)}, u32[]{:S(2)}, u32[]{:S(2)}) collective-permute-start(f32[512,256]{1,0:T(8,128)} %param.6), channel_id=1, source_target_pairs={{0,1},{1,0},{2,3},{3,2},{4,5},{5,4},{6,7},{7,6},{8,9},{9,8},{10,11... | collective-permute-start | bytes 1572872 | tf_op jit(solution)/shard_map/ppermute | solution.py:33
  0.0 7.5 %collective-permute-start.1 = (f32[512,256]{1,0:T(8,128)}, f32[512,256]{1,0:T(8,128)S(1)}, u32[]{:S(2)}, u32[]{:S(2)}) collective-permute-start(f32[512,256]{1,0:T(8,128)} %own_ref.3), channel_id=1, source_target_pairs={{0,1},{1,0},{2,3},{3,2},{4,5},{5,4},{6,7},{7,6},{8,9},{9,8},{10,11... | collective-permute-start | bytes 1572872 | tf_op jit(solution)/shard_map/ppermute | solution.py:33
  0.5 6.9 %collective-permute-start = (s32[2,1,64]{2,1,0:T(1,128)}, s32[2,1,64]{2,1,0:T(1,128)S(1)}, u32[]{:S(2)}, u32[]{:S(2)}) collective-permute-start(s32[2,1,64]{2,1,0:T(1,128)} %param.7), channel_id=1, source_target_pairs={{0,1},{1,2},{2,3},{3,4},{4,5},{5,6},{6,7},{7,0},{8,11},{9,12},{10,... | collective-permute-start | bytes 1544 | tf_op jit(solution)/shard_map/ppermute | solution.py:33
  2.7 4.1 %collective-permute-start.5 = (s32[2,1,64]{2,1,0:T(1,128)}, s32[2,1,64]{2,1,0:T(1,128)S(1)}, u32[]{:S(2)}, u32[]{:S(2)}) collective-permute-start(s32[2,1,64]{2,1,0:T(1,128)} %param.8), channel_id=1, source_target_pairs={{0,1},{1,8},{2,11},{3,18},{4,21},{5,28},{6,31},{7,6},{8,9},{9,16},... | collective-permute-start | bytes 1544 | tf_op jit(solution)/shard_map/ppermute | solution.py:33
  4.2 3.2 %copy-start = (f32[512,256]{1,0:T(8,128)S(1)}, f32[512,256]{1,0:T(8,128)}, u32[]{:S(2)}) copy-start(f32[512,256]{1,0:T(8,128)} %own_ref.3) | copy-start | bytes 1572868
  7.4 1.4 %copy-start.1 = (s32[2,1,64]{2,1,0:T(1,128)S(1)}, s32[2,1,64]{2,1,0:T(1,128)}, u32[]{:S(2)}) copy-start(s32[2,1,64]{2,1,0:T(1,128)} %param.8) | copy-start | bytes 1540
  7.4 3.0 %copy-start.2 = (s32[2,1,64]{2,1,0:T(1,128)S(1)}, s32[2,1,64]{2,1,0:T(1,128)}, u32[]{:S(2)}) copy-start(s32[2,1,64]{2,1,0:T(1,128)} %param.7) | copy-start | bytes 1540
  7.4 16.6 %collective-permute-start.7 = (f32[192,256]{1,0:T(8,128)S(1)}, f32[192,256]{1,0:T(8,128)S(1)}, u32[]{:S(2)}, u32[]{:S(2)}) collective-permute-start(f32[192,256]{1,0:T(8,128)S(1)} %shard_map.58), channel_id=1, source_target_pairs={{0,25},{1,0},{2,19},{3,26},{4,13},{5,20},{6,7},{7,14},{8,1},{9,8},... | collective-permute-start | bytes 589832 | tf_op jit(solution)/shard_map/ppermute | solution.py:33
  7.9 16.1 %collective-permute-start.2 = (f32[192,256]{1,0:T(8,128)S(1)}, f32[192,256]{1,0:T(8,128)S(1)}, u32[]{:S(2)}, u32[]{:S(2)}) collective-permute-start(f32[192,256]{1,0:T(8,128)S(1)} %shard_map.56), channel_id=1, source_target_pairs={{0,7},{1,0},{2,1},{3,2},{4,3},{5,4},{6,5},{7,6},{8,13},{9,14},{10,... | collective-permute-start | bytes 589832 | tf_op jit(solution)/shard_map/ppermute | solution.py:33
  8.7 3.5 %collective-permute-start.8 = (s32[2,1,64]{2,1,0:T(1,128)S(1)}, s32[2,1,64]{2,1,0:T(1,128)S(1)}, u32[]{:S(2)}, u32[]{:S(2)}) collective-permute-start(s32[2,1,64]{2,1,0:T(1,128)S(1)} %copy-done.1), channel_id=1, source_target_pairs={{0,9},{1,0},{2,19},{3,10},{4,29},{5,20},{6,7},{7,30},{8,17},{9,8},... | collective-permute-start | bytes 1544 | tf_op jit(solution)/shard_map/ppermute | solution.py:33
  10.4 7.8 %collective-permute-start.3 = (s32[2,1,64]{2,1,0:T(1,128)S(1)}, s32[2,1,64]{2,1,0:T(1,128)S(1)}, u32[]{:S(2)}, u32[]{:S(2)}) collective-permute-start(s32[2,1,64]{2,1,0:T(1,128)S(1)} %copy-done.2), channel_id=1, source_target_pairs={{0,3},{1,0},{2,5},{3,2},{4,7},{5,4},{6,1},{7,6},{8,13},{9,10},{10,... | collective-permute-start | bytes 1544 | tf_op jit(solution)/shard_map/ppermute | solution.py:33
  12.5 6.7 %collective-permute-start.9 = (f32[64,256]{1,0:T(8,128)S(1)}, f32[64,256]{1,0:T(8,128)S(1)}, u32[]{:S(2)}, u32[]{:S(2)}) collective-permute-start(f32[64,256]{1,0:T(8,128)S(1)} %shard_map.59), channel_id=1, source_target_pairs={{0,1},{1,24},{2,27},{3,18},{4,21},{5,12},{6,15},{7,6},{8,9},{9,0},... | collective-permute-start | bytes 196616 | tf_op jit(solution)/shard_map/ppermute | solution.py:33
  18.5 0.7 %copy-start.3 = (s32[2,1]{0,1:T(1,128)S(1)}, s32[2,1]{0,1:T(1,128)}, u32[]{:S(2)}) copy-start(s32[2,1]{0,1:T(1,128)} %param.9) | copy-start | bytes 28
  18.5 5.5 %collective-permute-start.4 = (f32[64,256]{1,0:T(8,128)S(1)}, f32[64,256]{1,0:T(8,128)S(1)}, u32[]{:S(2)}, u32[]{:S(2)}) collective-permute-start(f32[64,256]{1,0:T(8,128)S(1)} %shard_map.57), channel_id=1, source_target_pairs={{0,1},{1,6},{2,3},{3,0},{4,5},{5,2},{6,7},{7,4},{8,15},{9,12},{10,... | collective-permute-start | bytes 196616 | tf_op jit(solution)/shard_map/ppermute | solution.py:33
where the time goes:
time: 24.9 us; the launch traced here: 24.7 us
  waiting for transfers between devices  11.7 us (47%)
  starting transfers between devices  10.1 us (41%)
  Pallas kernels  2.11 us (8%)
  local copies, waits for them, and re-layouts  0.7 us (3%)
    ppermute x10, waiting for transfers between devices, send(): return lax.ppermute(shard, AXES, pairs)  11.7 us
    ppermute x10, starting transfers between devices, send(): return lax.ppermute(shard, AXES, pairs)  10.1 us
    pallas_call x6, Pallas kernels, call(): pl.pallas_call(kernel, out_shape=[jax.ShapeDtypeStruct(shape, jnp.float32...  2.11 us
    unnamed x8, local copies, waits for them, and re-layouts  0.61 us
  transfers between devices with their start and end apart: 10, of which 3 were waited for; matrix products, arithmetic and copies ran while one was open for 0% of the time, Pallas kernels for 6%

commit v1 on v0

--- a/solution.py
+++ b/solution.py
@@ -99,7 +99,26 @@
     return jnp.sum(spread, axis=0, keepdims=True)
 
 
-def finish_kernel(x_main, x_spare, z_main, z_spare, count_ref, eye_ref, out_ref):
+def dots(spare, a, side, x_ref, z_ref, slots):
+    products = []
+    for n, term in enumerate(terms_of(side)[spare]):
+        if term[0] == a:
+            at = slice(n * slots, (n + 1) * slots)
+            products.append(x_ref[at, :] * z_ref[at, :])
+    return sum(products[1:], products[0]) if products else None
+
+
+def part_kernel(x_main, z_main, eye_ref, out_ref):
+    slots = out_ref.shape[2]
+    eye = eye_ref[...] > 0
+
+    @by_side
+    def _(side):
+        for a in range(2):
+            out_ref[a] = line(dots(0, a, side, x_main, z_main, slots), eye)
+
+
+def finish_kernel(part_ref, x_spare, z_spare, count_ref, eye_ref, out_ref):
     slots = out_ref.shape[2]
     slot = lax.broadcasted_iota(jnp.int32, (1, slots), 1)
     eye = eye_ref[...] > 0
@@ -107,13 +126,11 @@
     @by_side
     def _(side):
         for a in range(2):
-            products = []
-            for terms, x_ref, z_ref in zip(terms_of(side), (x_main, x_spare), (z_main, z_spare)):
-                for n, term in enumerate(terms):
-                    if term[0] == a:
-                        at = slice(n * slots, (n + 1) * slots)
-                        products.append(x_ref[at, :] * z_ref[at, :])
-            out_ref[a] = jnp.where(slot < count_ref[a], line(sum(products[1:], products[0]), eye), 0.0)
+            value = part_ref[a]
+            more = dots(1, a, side, x_spare, z_spare, slots)
+            if more is not None:
+                value = value + line(more, eye)
+            out_ref[a] = jnp.where(slot < count_ref[a], value, 0.0)
 
 
 def call(kernel, shapes, *operands, cost=None):
@@ -157,7 +174,8 @@
         (columns,) = call(functools.partial(gather_kernel, spare, False), shape, dst, eye, z_partner, eye)
         z_got.append(send(columns, reply_z(spare)))
     count = edge_count.reshape(2, 1, 1)
-    (out,) = call(finish_kernel, [(2, 1, slots)], *x_got, *z_got, count, eye)
+    (part,) = call(part_kernel, [(2, 1, slots)], x_got[0], z_got[0], eye)
+    (out,) = call(finish_kernel, [(2, 1, slots)], part, x_got[1], z_got[1], count, eye)
     return out
 
 

time: 24.9 us -> 24.8 us (level)
    pallas_call x6 -> x7, Pallas kernels: 2.11 us -> 2.2 us  [call(): pl.pallas_call(kernel, out_shape=[jax.ShapeDtypeStruct(shape, jnp.float32...]
where the time goes in v1:
time: 24.8 us; the launch traced here: 24.7 us
  waiting for transfers between devices  11.6 us (47%)
  starting transfers between devices  10.1 us (41%)
  Pallas kernels  2.2 us (9%)
  local copies, waits for them, and re-layouts  0.7 us (3%)
    ppermute x10, waiting for transfers between devices, send(): return lax.ppermute(shard, AXES, pairs)  11.6 us
    ppermute x10, starting transfers between devices, send(): return lax.ppermute(shard, AXES, pairs)  10.1 us
    pallas_call x7, Pallas kernels, call(): pl.pallas_call(kernel, out_shape=[jax.ShapeDtypeStruct(shape, jnp.float32...  2.2 us
    unnamed x8, local copies, waits for them, and re-layouts  0.61 us
  transfers between devices with their start and end apart: 10, of which 3 were waited for; matrix products, arithmetic and copies ran while one was open for 0% of the time, Pallas kernels for 6%

profile of v1, /device:TPU:4, one launch (start us, length us, event | category | flops | bytes accessed | tf_op | source)
XLA Modules:
  0.0 24.7 jit_solution(8021319108290633691)
XLA Ops:
  0.0 0.0 collective-permute-start.4
  0.0 0.5 %collective-permute-start.1 = (f32[512,256]{1,0:T(8,128)}, f32[512,256]{1,0:T(8,128)S(1)}, u32[]{:S(2)}, u32[]{:S(2)}) collective-permute-start(f32[512,256]{1,0:T(8,128)} %own_ref.3), channel_id=1, source_target_pairs={{0,1},{1,0},{2,3},{3,2},{4,5},{5,4},{6,7},{7,6},{8,9},{9,8},{10,11... | collective-permute-start | bytes 1572872 | tf_op jit(solution)/shard_map/ppermute | solution.py:33
  0.5 2.2 %collective-permute-start = (s32[2,1,64]{2,1,0:T(1,128)}, s32[2,1,64]{2,1,0:T(1,128)S(1)}, u32[]{:S(2)}, u32[]{:S(2)}) collective-permute-start(s32[2,1,64]{2,1,0:T(1,128)} %param.7), channel_id=1, source_target_pairs={{0,1},{1,2},{2,3},{3,4},{4,5},{5,6},{6,7},{7,0},{8,11},{9,12},{10,... | collective-permute-start | bytes 1544 | tf_op jit(solution)/shard_map/ppermute | solution.py:33
  2.7 1.5 %collective-permute-start.3 = (s32[2,1,64]{2,1,0:T(1,128)}, s32[2,1,64]{2,1,0:T(1,128)S(1)}, u32[]{:S(2)}, u32[]{:S(2)}) collective-permute-start(s32[2,1,64]{2,1,0:T(1,128)} %param.8), channel_id=1, source_target_pairs={{0,1},{1,8},{2,11},{3,18},{4,21},{5,28},{6,31},{7,6},{8,9},{9,16},... | collective-permute-start | bytes 1544 | tf_op jit(solution)/shard_map/ppermute | solution.py:33
  4.2 0.0 copy-start
  4.2 2.6 %collective-permute-done.3.index_ref = s32[2,1,64]{2,1,0:T(1,128)S(1)} collective-permute-done((s32[2,1,64]{2,1,0:T(1,128)}, s32[2,1,64]{2,1,0:T(1,128)S(1)}, u32[]{:S(2)}, u32[]{:S(2)}) %collective-permute-start.3) | collective-permute-done | bytes 544 | tf_op jit(solution)/shard_map/ppermute | solution.py:33
  6.8 0.0 collective-permute-done.4.partner_ref
  6.8 0.5 %shard_map.57 = f32[192,256]{1,0:T(8,128)S(1)} custom-call(s32[2,1,64]{2,1,0:T(1,128)S(1)} %collective-permute-done.3.index_ref, f32[64,64]{1,0:T(8,128)S(1)} %shard_map.55.eye_ref.own_ref, f32[512,256]{1,0:T(8,128)S(1)} %collective-permute-done.4.partner_ref, f32[64,64]{1,0:T(8,128)S(1)} %shard_map.55.eye_ref.own_ref), custom_call_target="tpu_custom_call" | custom-call | tf_op jit(solution)/shard_map/pallas_call | solution.py:137
  7.4 0.0 copy-start.1
  7.4 0.0 copy-start.2
  7.4 0.1 collective-permute-start.5
  7.4 0.0 collective-permute-done.index_ref
  7.5 0.0 collective-permute-done.1.partner_ref
  7.5 0.0 copy-done
  7.5 0.4 %shard_map.56 = f32[192,256]{1,0:T(8,128)S(1)} custom-call(s32[2,1,64]{2,1,0:T(1,128)S(1)} %collective-permute-done.index_ref, f32[512,256]{1,0:T(8,128)S(1)} %copy-done, f32[512,256]{1,0:T(8,128)S(1)} %collective-permute-done.1.partner_ref, f32[64,64]{1,0:T(8,128)S(1)} %shard_map.55.eye_ref.own_ref), custom_call_target="tpu_custom_call" | custom-call | tf_op jit(solution)/shard_map/pallas_call | solution.py:137
  7.9 0.8 %collective-permute-start.2 = (f32[192,256]{1,0:T(8,128)S(1)}, f32[192,256]{1,0:T(8,128)S(1)}, u32[]{:S(2)}, u32[]{:S(2)}) collective-permute-start(f32[192,256]{1,0:T(8,128)S(1)} %shard_map.56), channel_id=1, source_target_pairs={{0,7},{1,0},{2,1},{3,2},{4,3},{5,4},{6,5},{7,6},{8,13},{9,14},{10,... | collective-permute-start | bytes 589832 | tf_op jit(solution)/shard_map/ppermute | solution.py:33
  8.7 0.0 copy-done.1
  8.7 1.7 %collective-permute-start.8 = (s32[2,1,64]{2,1,0:T(1,128)S(1)}, s32[2,1,64]{2,1,0:T(1,128)S(1)}, u32[]{:S(2)}, u32[]{:S(2)}) collective-permute-start(s32[2,1,64]{2,1,0:T(1,128)S(1)} %copy-done.1), channel_id=1, source_target_pairs={{0,9},{1,0},{2,19},{3,10},{4,29},{5,20},{6,7},{7,30},{8,17},{9,8},... | collective-permute-start | bytes 1544 | tf_op jit(solution)/shard_map/ppermute | solution.py:33
  10.4 0.0 copy-done.2
  10.4 1.8 %collective-permute-start.6 = (s32[2,1,64]{2,1,0:T(1,128)S(1)}, s32[2,1,64]{2,1,0:T(1,128)S(1)}, u32[]{:S(2)}, u32[]{:S(2)}) collective-permute-start(s32[2,1,64]{2,1,0:T(1,128)S(1)} %copy-done.2), channel_id=1, source_target_pairs={{0,3},{1,0},{2,5},{3,2},{4,7},{5,4},{6,1},{7,6},{8,13},{9,10},{10,... | collective-permute-start | bytes 1544 | tf_op jit(solution)/shard_map/ppermute | solution.py:33
  12.3 0.0 collective-permute-done.8.index_ref
  12.3 0.2 shard_map.60
  12.5 1.4 %collective-permute-start.9 = (f32[64,256]{1,0:T(8,128)S(1)}, f32[64,256]{1,0:T(8,128)S(1)}, u32[]{:S(2)}, u32[]{:S(2)}) collective-permute-start(f32[64,256]{1,0:T(8,128)S(1)} %shard_map.60), channel_id=1, source_target_pairs={{0,1},{1,24},{2,27},{3,18},{4,21},{5,12},{6,15},{7,6},{8,9},{9,0},... | collective-permute-start | bytes 196616 | tf_op jit(solution)/shard_map/ppermute | solution.py:33
  13.9 4.3 %collective-permute-done.6.index_ref = s32[2,1,64]{2,1,0:T(1,128)S(1)} collective-permute-done((s32[2,1,64]{2,1,0:T(1,128)S(1)}, s32[2,1,64]{2,1,0:T(1,128)S(1)}, u32[]{:S(2)}, u32[]{:S(2)}) %collective-permute-start.6) | collective-permute-done | bytes 544 | tf_op jit(solution)/shard_map/ppermute | solution.py:33
  18.2 0.2 shard_map.59
  18.5 0.0 copy-start.3
  18.5 0.1 collective-permute-start.7
  18.5 0.6 %copy-done.3 = s32[2,1]{0,1:T(1,128)S(1)} copy-done((s32[2,1]{0,1:T(1,128)S(1)}, s32[2,1]{0,1:T(1,128)}, u32[]{:S(2)}) %copy-start.3) | copy-done | bytes 32
  19.1 0.1 copy.6.count_ref
  19.2 0.0 collective-permute-done.5.z_main
  19.2 0.0 collective-permute-done.2.x_main
  19.2 0.1 shard_map.58.part_ref
  19.3 0.0 collective-permute-done.9.z_spare
  19.4 4.7 %collective-permute-done.7.x_spare = f32[64,256]{1,0:T(8,128)S(1)} collective-permute-done((f32[64,256]{1,0:T(8,128)S(1)}, f32[64,256]{1,0:T(8,128)S(1)}, u32[]{:S(2)}, u32[]{:S(2)}) %collective-permute-start.7) | collective-permute-done | bytes 65568 | tf_op jit(solution)/shard_map/ppermute | solution.py:33
  24.0 0.7 %shard_map.61 = f32[2,1,64]{2,1,0:T(1,128)} custom-call(f32[2,1,64]{2,1,0:T(1,128)S(1)} %shard_map.58.part_ref, f32[64,256]{1,0:T(8,128)S(1)} %collective-permute-done.7.x_spare, f32[64,256]{1,0:T(8,128)S(1)} %collective-permute-done.9.z_spare, s32[2,1,1]{2,1,0:T(1,128)S(1)} %copy.6.count_ref, f32[64,64]{1,0:T(8,128)S(1)} %shard_map.55.eye_ref.own_ref), custom_call_target="tpu_custom_call" | custom-call | tf_op jit(solution)/shard_map/pallas_call | solution.py:137
  (1 shorter events, 0.0 us)
Async XLA Ops:
  0.0 6.8 %collective-permute-start.4 = (f32[512,256]{1,0:T(8,128)}, f32[512,256]{1,0:T(8,128)S(1)}, u32[]{:S(2)}, u32[]{:S(2)}) collective-permute-start(f32[512,256]{1,0:T(8,128)} %param.6), channel_id=1, source_target_pairs={{0,1},{1,0},{2,3},{3,2},{4,5},{5,4},{6,7},{7,6},{8,9},{9,8},{10,11... | collective-permute-start | bytes 1572872 | tf_op jit(solution)/shard_map/ppermute | solution.py:33
  0.0 7.5 %collective-permute-start.1 = (f32[512,256]{1,0:T(8,128)}, f32[512,256]{1,0:T(8,128)S(1)}, u32[]{:S(2)}, u32[]{:S(2)}) collective-permute-start(f32[512,256]{1,0:T(8,128)} %own_ref.3), channel_id=1, source_target_pairs={{0,1},{1,0},{2,3},{3,2},{4,5},{5,4},{6,7},{7,6},{8,9},{9,8},{10,11... | collective-permute-start | bytes 1572872 | tf_op jit(solution)/shard_map/ppermute | solution.py:33
  0.5 6.9 %collective-permute-start = (s32[2,1,64]{2,1,0:T(1,128)}, s32[2,1,64]{2,1,0:T(1,128)S(1)}, u32[]{:S(2)}, u32[]{:S(2)}) collective-permute-start(s32[2,1,64]{2,1,0:T(1,128)} %param.7), channel_id=1, source_target_pairs={{0,1},{1,2},{2,3},{3,4},{4,5},{5,6},{6,7},{7,0},{8,11},{9,12},{10,... | collective-permute-start | bytes 1544 | tf_op jit(solution)/shard_map/ppermute | solution.py:33
  2.7 4.1 %collective-permute-start.3 = (s32[2,1,64]{2,1,0:T(1,128)}, s32[2,1,64]{2,1,0:T(1,128)S(1)}, u32[]{:S(2)}, u32[]{:S(2)}) collective-permute-start(s32[2,1,64]{2,1,0:T(1,128)} %param.8), channel_id=1, source_target_pairs={{0,1},{1,8},{2,11},{3,18},{4,21},{5,28},{6,31},{7,6},{8,9},{9,16},... | collective-permute-start | bytes 1544 | tf_op jit(solution)/shard_map/ppermute | solution.py:33
  4.2 3.2 %copy-start = (f32[512,256]{1,0:T(8,128)S(1)}, f32[512,256]{1,0:T(8,128)}, u32[]{:S(2)}) copy-start(f32[512,256]{1,0:T(8,128)} %own_ref.3) | copy-start | bytes 1572868
  7.4 1.4 %copy-start.1 = (s32[2,1,64]{2,1,0:T(1,128)S(1)}, s32[2,1,64]{2,1,0:T(1,128)}, u32[]{:S(2)}) copy-start(s32[2,1,64]{2,1,0:T(1,128)} %param.8) | copy-start | bytes 1540
  7.4 3.0 %copy-start.2 = (s32[2,1,64]{2,1,0:T(1,128)S(1)}, s32[2,1,64]{2,1,0:T(1,128)}, u32[]{:S(2)}) copy-start(s32[2,1,64]{2,1,0:T(1,128)} %param.7) | copy-start | bytes 1540
  7.4 11.8 %collective-permute-start.5 = (f32[192,256]{1,0:T(8,128)S(1)}, f32[192,256]{1,0:T(8,128)S(1)}, u32[]{:S(2)}, u32[]{:S(2)}) collective-permute-start(f32[192,256]{1,0:T(8,128)S(1)} %shard_map.57), channel_id=1, source_target_pairs={{0,25},{1,0},{2,19},{3,26},{4,13},{5,20},{6,7},{7,14},{8,1},{9,8},... | collective-permute-start | bytes 589832 | tf_op jit(solution)/shard_map/ppermute | solution.py:33
  7.9 11.3 %collective-permute-start.2 = (f32[192,256]{1,0:T(8,128)S(1)}, f32[192,256]{1,0:T(8,128)S(1)}, u32[]{:S(2)}, u32[]{:S(2)}) collective-permute-start(f32[192,256]{1,0:T(8,128)S(1)} %shard_map.56), channel_id=1, source_target_pairs={{0,7},{1,0},{2,1},{3,2},{4,3},{5,4},{6,5},{7,6},{8,13},{9,14},{10,... | collective-permute-start | bytes 589832 | tf_op jit(solution)/shard_map/ppermute | solution.py:33
  8.7 3.5 %collective-permute-start.8 = (s32[2,1,64]{2,1,0:T(1,128)S(1)}, s32[2,1,64]{2,1,0:T(1,128)S(1)}, u32[]{:S(2)}, u32[]{:S(2)}) collective-permute-start(s32[2,1,64]{2,1,0:T(1,128)S(1)} %copy-done.1), channel_id=1, source_target_pairs={{0,9},{1,0},{2,19},{3,10},{4,29},{5,20},{6,7},{7,30},{8,17},{9,8},... | collective-permute-start | bytes 1544 | tf_op jit(solution)/shard_map/ppermute | solution.py:33
  10.4 7.8 %collective-permute-start.6 = (s32[2,1,64]{2,1,0:T(1,128)S(1)}, s32[2,1,64]{2,1,0:T(1,128)S(1)}, u32[]{:S(2)}, u32[]{:S(2)}) collective-permute-start(s32[2,1,64]{2,1,0:T(1,128)S(1)} %copy-done.2), channel_id=1, source_target_pairs={{0,3},{1,0},{2,5},{3,2},{4,7},{5,4},{6,1},{7,6},{8,13},{9,10},{10,... | collective-permute-start | bytes 1544 | tf_op jit(solution)/shard_map/ppermute | solution.py:33
  12.5 6.8 %collective-permute-start.9 = (f32[64,256]{1,0:T(8,128)S(1)}, f32[64,256]{1,0:T(8,128)S(1)}, u32[]{:S(2)}, u32[]{:S(2)}) collective-permute-start(f32[64,256]{1,0:T(8,128)S(1)} %shard_map.60), channel_id=1, source_target_pairs={{0,1},{1,24},{2,27},{3,18},{4,21},{5,12},{6,15},{7,6},{8,9},{9,0},... | collective-permute-start | bytes 196616 | tf_op jit(solution)/shard_map/ppermute | solution.py:33
  18.5 0.7 %copy-start.3 = (s32[2,1]{0,1:T(1,128)S(1)}, s32[2,1]{0,1:T(1,128)}, u32[]{:S(2)}) copy-start(s32[2,1]{0,1:T(1,128)} %param.9) | copy-start | bytes 28
  18.5 5.5 %collective-permute-start.7 = (f32[64,256]{1,0:T(8,128)S(1)}, f32[64,256]{1,0:T(8,128)S(1)}, u32[]{:S(2)}, u32[]{:S(2)}) collective-permute-start(f32[64,256]{1,0:T(8,128)S(1)} %shard_map.59), channel_id=1, source_target_pairs={{0,1},{1,6},{2,3},{3,0},{4,5},{5,2},{6,7},{7,4},{8,15},{9,12},{10,... | collective-permute-start | bytes 196616 | tf_op jit(solution)/shard_map/ppermute | solution.py:33

commit v2 on v1

--- a/solution.py
+++ b/solution.py
@@ -53,14 +53,9 @@
     eye_ref[...] = diagonal(eye_ref.shape[0]).astype(jnp.float32)
 
 
-def pick(lines, width, eye):
-    columns = []
-    for line in lines:
-        slots = line.shape[1]
-        spread = jnp.where(eye, jnp.broadcast_to(line, (slots, slots)), 0)
-        columns.append(jnp.sum(spread, axis=1, keepdims=True))
-    column = jnp.concatenate(columns, axis=0)
-    chosen = column == lax.broadcasted_iota(jnp.int32, (column.shape[0], width), 1)
+def pick(lines, width):
+    line = jnp.concatenate(lines, axis=1)
+    chosen = line == lax.broadcasted_iota(jnp.int32, (width, line.shape[1]), 0)
     return chosen.astype(jnp.float32).astype(jnp.bfloat16)
 
 
@@ -73,7 +68,6 @@
 def gather_kernel(spare, of_x, index_ref, own_ref, partner_ref, eye_ref, out_ref):
     width = out_ref.shape[1]
     slots = index_ref.shape[2]
-    eye = eye_ref[...] > 0
 
     @by_side
     def _(side):
@@ -81,11 +75,11 @@
         for place, (a, g) in enumerate(terms_of(1 - side)[spare]):
             blocks.setdefault((g != side, a) if of_x else (True, g), []).append((place, a))
         for (partner, at), wanted in blocks.items():
-            chosen = pick([index_ref[a] for _, a in wanted], width, eye)
+            chosen = pick([index_ref[a] for _, a in wanted], width)
             block = (partner_ref if partner else own_ref)[at * width : (at + 1) * width, :]
             taken = sum(
                 lax.dot_general(
-                    chosen, piece, (((1,), (0 if of_x else 1,)), ((), ())), preferred_element_type=jnp.float32
+                    chosen, piece, (((0,), (0 if of_x else 1,)), ((), ())), preferred_element_type=jnp.float32
                 )
                 for piece in pieces(block)
             )

time: 24.8 us -> 24.7 us (level)
  no operation moved by 1% of the time
where the time goes in v2:
time: 24.7 us; the launch traced here: 24.6 us
  waiting for transfers between devices  11.5 us (47%)
  starting transfers between devices  10.1 us (41%)
  Pallas kernels  2.09 us (8%)
  local copies, waits for them, and re-layouts  0.7 us (3%)
    ppermute x10, waiting for transfers between devices, send(): return lax.ppermute(shard, AXES, pairs)  11.5 us
    ppermute x10, starting transfers between devices, send(): return lax.ppermute(shard, AXES, pairs)  10.1 us
    pallas_call x7, Pallas kernels, call(): pl.pallas_call(kernel, out_shape=[jax.ShapeDtypeStruct(shape, jnp.float32...  2.09 us
    unnamed x8, local copies, waits for them, and re-layouts  0.61 us
  transfers between devices with their start and end apart: 10, of which 3 were waited for; matrix products, arithmetic and copies ran while one was open for 0% of the time, Pallas kernels for 6%

profile of v2, /device:TPU:4, one launch (start us, length us, event | category | flops | bytes accessed | tf_op | source)
XLA Modules:
  0.0 24.6 jit_solution(12691315305706852355)
XLA Ops:
  0.0 0.0 collective-permute-start.4
  0.0 0.5 %collective-permute-start.1 = (f32[512,256]{1,0:T(8,128)}, f32[512,256]{1,0:T(8,128)S(1)}, u32[]{:S(2)}, u32[]{:S(2)}) collective-permute-start(f32[512,256]{1,0:T(8,128)} %own_ref.3), channel_id=1, source_target_pairs={{0,1},{1,0},{2,3},{3,2},{4,5},{5,4},{6,7},{7,6},{8,9},{9,8},{10,11... | collective-permute-start | bytes 1572872 | tf_op jit(solution)/shard_map/ppermute | solution.py:33
  0.5 2.2 %collective-permute-start = (s32[2,1,64]{2,1,0:T(1,128)}, s32[2,1,64]{2,1,0:T(1,128)S(1)}, u32[]{:S(2)}, u32[]{:S(2)}) collective-permute-start(s32[2,1,64]{2,1,0:T(1,128)} %param.7), channel_id=1, source_target_pairs={{0,1},{1,2},{2,3},{3,4},{4,5},{5,6},{6,7},{7,0},{8,11},{9,12},{10,... | collective-permute-start | bytes 1544 | tf_op jit(solution)/shard_map/ppermute | solution.py:33
  2.7 1.5 %collective-permute-start.3 = (s32[2,1,64]{2,1,0:T(1,128)}, s32[2,1,64]{2,1,0:T(1,128)S(1)}, u32[]{:S(2)}, u32[]{:S(2)}) collective-permute-start(s32[2,1,64]{2,1,0:T(1,128)} %param.8), channel_id=1, source_target_pairs={{0,1},{1,8},{2,11},{3,18},{4,21},{5,28},{6,31},{7,6},{8,9},{9,16},... | collective-permute-start | bytes 1544 | tf_op jit(solution)/shard_map/ppermute | solution.py:33
  4.2 0.0 copy-start
  4.2 2.6 %collective-permute-done.3.index_ref = s32[2,1,64]{2,1,0:T(1,128)S(1)} collective-permute-done((s32[2,1,64]{2,1,0:T(1,128)}, s32[2,1,64]{2,1,0:T(1,128)S(1)}, u32[]{:S(2)}, u32[]{:S(2)}) %collective-permute-start.3) | collective-permute-done | bytes 544 | tf_op jit(solution)/shard_map/ppermute | solution.py:33
  6.8 0.0 collective-permute-done.4.partner_ref
  6.8 0.4 %shard_map.57 = f32[192,256]{1,0:T(8,128)S(1)} custom-call(s32[2,1,64]{2,1,0:T(1,128)S(1)} %collective-permute-done.3.index_ref, f32[64,64]{1,0:T(8,128)S(1)} %shard_map.55.eye_ref.own_ref, f32[512,256]{1,0:T(8,128)S(1)} %collective-permute-done.4.partner_ref, f32[64,64]{1,0:T(8,128)S(1)} %shard_map.55.eye_ref.own_ref), custom_call_target="tpu_custom_call" | custom-call | tf_op jit(solution)/shard_map/pallas_call | solution.py:131
  7.3 0.0 copy-start.1
  7.3 0.0 copy-start.2
  7.3 0.1 collective-permute-start.5
  7.3 0.0 collective-permute-done.index_ref
  7.4 0.0 collective-permute-done.1.partner_ref
  7.4 0.0 copy-done
  7.4 0.4 %shard_map.56 = f32[192,256]{1,0:T(8,128)S(1)} custom-call(s32[2,1,64]{2,1,0:T(1,128)S(1)} %collective-permute-done.index_ref, f32[512,256]{1,0:T(8,128)S(1)} %copy-done, f32[512,256]{1,0:T(8,128)S(1)} %collective-permute-done.1.partner_ref, f32[64,64]{1,0:T(8,128)S(1)} %shard_map.55.eye_ref.own_ref), custom_call_target="tpu_custom_call" | custom-call | tf_op jit(solution)/shard_map/pallas_call | solution.py:131
  7.8 0.8 %collective-permute-start.2 = (f32[192,256]{1,0:T(8,128)S(1)}, f32[192,256]{1,0:T(8,128)S(1)}, u32[]{:S(2)}, u32[]{:S(2)}) collective-permute-start(f32[192,256]{1,0:T(8,128)S(1)} %shard_map.56), channel_id=1, source_target_pairs={{0,7},{1,0},{2,1},{3,2},{4,3},{5,4},{6,5},{7,6},{8,13},{9,14},{10,... | collective-permute-start | bytes 589832 | tf_op jit(solution)/shard_map/ppermute | solution.py:33
  8.6 0.0 copy-done.1
  8.6 1.7 %collective-permute-start.8 = (s32[2,1,64]{2,1,0:T(1,128)S(1)}, s32[2,1,64]{2,1,0:T(1,128)S(1)}, u32[]{:S(2)}, u32[]{:S(2)}) collective-permute-start(s32[2,1,64]{2,1,0:T(1,128)S(1)} %copy-done.1), channel_id=1, source_target_pairs={{0,9},{1,0},{2,19},{3,10},{4,29},{5,20},{6,7},{7,30},{8,17},{9,8},... | collective-permute-start | bytes 1544 | tf_op jit(solution)/shard_map/ppermute | solution.py:33
  10.3 0.0 copy-done.2
  10.3 1.9 %collective-permute-start.6 = (s32[2,1,64]{2,1,0:T(1,128)S(1)}, s32[2,1,64]{2,1,0:T(1,128)S(1)}, u32[]{:S(2)}, u32[]{:S(2)}) collective-permute-start(s32[2,1,64]{2,1,0:T(1,128)S(1)} %copy-done.2), channel_id=1, source_target_pairs={{0,3},{1,0},{2,5},{3,2},{4,7},{5,4},{6,1},{7,6},{8,13},{9,10},{10,... | collective-permute-start | bytes 1544 | tf_op jit(solution)/shard_map/ppermute | solution.py:33
  12.2 0.0 collective-permute-done.8.index_ref
  12.2 0.3 %shard_map.60 = f32[64,256]{1,0:T(8,128)S(1)} custom-call(s32[2,1,64]{2,1,0:T(1,128)S(1)} %collective-permute-done.8.index_ref, f32[64,64]{1,0:T(8,128)S(1)} %shard_map.55.eye_ref.own_ref, f32[512,256]{1,0:T(8,128)S(1)} %collective-permute-done.4.partner_ref, f32[64,64]{1,0:T(8,128)S(1)} %shard_map.55.eye_ref.own_ref), custom_call_target="tpu_custom_call" | custom-call | tf_op jit(solution)/shard_map/pallas_call | solution.py:131
  12.4 1.4 %collective-permute-start.9 = (f32[64,256]{1,0:T(8,128)S(1)}, f32[64,256]{1,0:T(8,128)S(1)}, u32[]{:S(2)}, u32[]{:S(2)}) collective-permute-start(f32[64,256]{1,0:T(8,128)S(1)} %shard_map.60), channel_id=1, source_target_pairs={{0,1},{1,24},{2,27},{3,18},{4,21},{5,12},{6,15},{7,6},{8,9},{9,0},... | collective-permute-start | bytes 196616 | tf_op jit(solution)/shard_map/ppermute | solution.py:33
  13.8 4.3 %collective-permute-done.6.index_ref = s32[2,1,64]{2,1,0:T(1,128)S(1)} collective-permute-done((s32[2,1,64]{2,1,0:T(1,128)S(1)}, s32[2,1,64]{2,1,0:T(1,128)S(1)}, u32[]{:S(2)}, u32[]{:S(2)}) %collective-permute-start.6) | collective-permute-done | bytes 544 | tf_op jit(solution)/shard_map/ppermute | solution.py:33
  18.1 0.2 shard_map.59
  18.3 0.0 copy-start.3
  18.3 0.1 collective-permute-start.7
  18.4 0.6 %copy-done.3 = s32[2,1]{0,1:T(1,128)S(1)} copy-done((s32[2,1]{0,1:T(1,128)S(1)}, s32[2,1]{0,1:T(1,128)}, u32[]{:S(2)}) %copy-start.3) | copy-done | bytes 32
  19.0 0.1 copy.6.count_ref
  19.1 0.0 collective-permute-done.5.z_main
  19.1 0.0 collective-permute-done.2.x_main
  19.1 0.1 shard_map.58.part_ref
  19.2 0.0 collective-permute-done.9.z_spare
  19.2 4.7 %collective-permute-done.7.x_spare = f32[64,256]{1,0:T(8,128)S(1)} collective-permute-done((f32[64,256]{1,0:T(8,128)S(1)}, f32[64,256]{1,0:T(8,128)S(1)}, u32[]{:S(2)}, u32[]{:S(2)}) %collective-permute-start.7) | collective-permute-done | bytes 65568 | tf_op jit(solution)/shard_map/ppermute | solution.py:33
  23.9 0.7 %shard_map.61 = f32[2,1,64]{2,1,0:T(1,128)} custom-call(f32[2,1,64]{2,1,0:T(1,128)S(1)} %shard_map.58.part_ref, f32[64,256]{1,0:T(8,128)S(1)} %collective-permute-done.7.x_spare, f32[64,256]{1,0:T(8,128)S(1)} %collective-permute-done.9.z_spare, s32[2,1,1]{2,1,0:T(1,128)S(1)} %copy.6.count_ref, f32[64,64]{1,0:T(8,128)S(1)} %shard_map.55.eye_ref.own_ref), custom_call_target="tpu_custom_call" | custom-call | tf_op jit(solution)/shard_map/pallas_call | solution.py:131
  (1 shorter events, 0.0 us)
Async XLA Ops:
  0.0 6.8 %collective-permute-start.4 = (f32[512,256]{1,0:T(8,128)}, f32[512,256]{1,0:T(8,128)S(1)}, u32[]{:S(2)}, u32[]{:S(2)}) collective-permute-start(f32[512,256]{1,0:T(8,128)} %param.6), channel_id=1, source_target_pairs={{0,1},{1,0},{2,3},{3,2},{4,5},{5,4},{6,7},{7,6},{8,9},{9,8},{10,11... | collective-permute-start | bytes 1572872 | tf_op jit(solution)/shard_map/ppermute | solution.py:33
  0.0 7.4 %collective-permute-start.1 = (f32[512,256]{1,0:T(8,128)}, f32[512,256]{1,0:T(8,128)S(1)}, u32[]{:S(2)}, u32[]{:S(2)}) collective-permute-start(f32[512,256]{1,0:T(8,128)} %own_ref.3), channel_id=1, source_target_pairs={{0,1},{1,0},{2,3},{3,2},{4,5},{5,4},{6,7},{7,6},{8,9},{9,8},{10,11... | collective-permute-start | bytes 1572872 | tf_op jit(solution)/shard_map/ppermute | solution.py:33
  0.5 6.8 %collective-permute-start = (s32[2,1,64]{2,1,0:T(1,128)}, s32[2,1,64]{2,1,0:T(1,128)S(1)}, u32[]{:S(2)}, u32[]{:S(2)}) collective-permute-start(s32[2,1,64]{2,1,0:T(1,128)} %param.7), channel_id=1, source_target_pairs={{0,1},{1,2},{2,3},{3,4},{4,5},{5,6},{6,7},{7,0},{8,11},{9,12},{10,... | collective-permute-start | bytes 1544 | tf_op jit(solution)/shard_map/ppermute | solution.py:33
  2.7 4.1 %collective-permute-start.3 = (s32[2,1,64]{2,1,0:T(1,128)}, s32[2,1,64]{2,1,0:T(1,128)S(1)}, u32[]{:S(2)}, u32[]{:S(2)}) collective-permute-start(s32[2,1,64]{2,1,0:T(1,128)} %param.8), channel_id=1, source_target_pairs={{0,1},{1,8},{2,11},{3,18},{4,21},{5,28},{6,31},{7,6},{8,9},{9,16},... | collective-permute-start | bytes 1544 | tf_op jit(solution)/shard_map/ppermute | solution.py:33
  4.2 3.1 %copy-start = (f32[512,256]{1,0:T(8,128)S(1)}, f32[512,256]{1,0:T(8,128)}, u32[]{:S(2)}) copy-start(f32[512,256]{1,0:T(8,128)} %own_ref.3) | copy-start | bytes 1572868
  7.3 1.4 %copy-start.1 = (s32[2,1,64]{2,1,0:T(1,128)S(1)}, s32[2,1,64]{2,1,0:T(1,128)}, u32[]{:S(2)}) copy-start(s32[2,1,64]{2,1,0:T(1,128)} %param.8) | copy-start | bytes 1540
  7.3 3.0 %copy-start.2 = (s32[2,1,64]{2,1,0:T(1,128)S(1)}, s32[2,1,64]{2,1,0:T(1,128)}, u32[]{:S(2)}) copy-start(s32[2,1,64]{2,1,0:T(1,128)} %param.7) | copy-start | bytes 1540
  7.3 11.8 %collective-permute-start.5 = (f32[192,256]{1,0:T(8,128)S(1)}, f32[192,256]{1,0:T(8,128)S(1)}, u32[]{:S(2)}, u32[]{:S(2)}) collective-permute-start(f32[192,256]{1,0:T(8,128)S(1)} %shard_map.57), channel_id=1, source_target_pairs={{0,25},{1,0},{2,19},{3,26},{4,13},{5,20},{6,7},{7,14},{8,1},{9,8},... | collective-permute-start | bytes 589832 | tf_op jit(solution)/shard_map/ppermute | solution.py:33
  7.8 11.3 %collective-permute-start.2 = (f32[192,256]{1,0:T(8,128)S(1)}, f32[192,256]{1,0:T(8,128)S(1)}, u32[]{:S(2)}, u32[]{:S(2)}) collective-permute-start(f32[192,256]{1,0:T(8,128)S(1)} %shard_map.56), channel_id=1, source_target_pairs={{0,7},{1,0},{2,1},{3,2},{4,3},{5,4},{6,5},{7,6},{8,13},{9,14},{10,... | collective-permute-start | bytes 589832 | tf_op jit(solution)/shard_map/ppermute | solution.py:33
  8.6 3.5 %collective-permute-start.8 = (s32[2,1,64]{2,1,0:T(1,128)S(1)}, s32[2,1,64]{2,1,0:T(1,128)S(1)}, u32[]{:S(2)}, u32[]{:S(2)}) collective-permute-start(s32[2,1,64]{2,1,0:T(1,128)S(1)} %copy-done.1), channel_id=1, source_target_pairs={{0,9},{1,0},{2,19},{3,10},{4,29},{5,20},{6,7},{7,30},{8,17},{9,8},... | collective-permute-start | bytes 1544 | tf_op jit(solution)/shard_map/ppermute | solution.py:33
  10.3 7.8 %collective-permute-start.6 = (s32[2,1,64]{2,1,0:T(1,128)S(1)}, s32[2,1,64]{2,1,0:T(1,128)S(1)}, u32[]{:S(2)}, u32[]{:S(2)}) collective-permute-start(s32[2,1,64]{2,1,0:T(1,128)S(1)} %copy-done.2), channel_id=1, source_target_pairs={{0,3},{1,0},{2,5},{3,2},{4,7},{5,4},{6,1},{7,6},{8,13},{9,10},{10,... | collective-permute-start | bytes 1544 | tf_op jit(solution)/shard_map/ppermute | solution.py:33
  12.4 6.8 %collective-permute-start.9 = (f32[64,256]{1,0:T(8,128)S(1)}, f32[64,256]{1,0:T(8,128)S(1)}, u32[]{:S(2)}, u32[]{:S(2)}) collective-permute-start(f32[64,256]{1,0:T(8,128)S(1)} %shard_map.60), channel_id=1, source_target_pairs={{0,1},{1,24},{2,27},{3,18},{4,21},{5,12},{6,15},{7,6},{8,9},{9,0},... | collective-permute-start | bytes 196616 | tf_op jit(solution)/shard_map/ppermute | solution.py:33
  18.3 0.7 %copy-start.3 = (s32[2,1]{0,1:T(1,128)S(1)}, s32[2,1]{0,1:T(1,128)}, u32[]{:S(2)}) copy-start(s32[2,1]{0,1:T(1,128)} %param.9) | copy-start | bytes 28
  18.3 5.5 %collective-permute-start.7 = (f32[64,256]{1,0:T(8,128)S(1)}, f32[64,256]{1,0:T(8,128)S(1)}, u32[]{:S(2)}, u32[]{:S(2)}) collective-permute-start(f32[64,256]{1,0:T(8,128)S(1)} %shard_map.59), channel_id=1, source_target_pairs={{0,1},{1,6},{2,3},{3,0},{4,5},{5,2},{6,7},{7,4},{8,15},{9,12},{10,... | collective-permute-start | bytes 196616 | tf_op jit(solution)/shard_map/ppermute | solution.py:33
